TPU v7x, 32 devices: a whole 2x2x4 slice. The times are simulated.
32 devices in a mesh: trial: 2 (over core), qa: 4 (over y, x), qb: 4 (over z).
Axes of the slice: x: 2, y: 2, z: 4, core: 2. Of those that a mesh axis runs over, the one named last changes fastest.
Arguments:
- wave_parts: float32 [4, 64, 128, 128], P('trial', ('qa', 'qb')), parts along dimension 0, may hold values from -6 to 6
- level_table: float32 [128, 128, 128], P(('trial', 'qa', 'qb')), parts along dimension 0, may hold values from -2 to 2
- diagonal_angles: float32 [6, 128], P('trial'), parts along dimension 0, may hold values from 0.3 to 1.2
- turn_angles: float32 [6, 4], P('trial'), parts along dimension 0, may hold values from 0.3 to 1.2
Outputs:
- final_parts: float32 [4, 64, 128, 128], P('trial', ('qa', 'qb')), parts along dimension 0
There are 2 independent parts, one for each index of `trial`. A program takes and returns all parts, laid end to end along the dimension named above; each array names one. Nothing has to cross between parts.
All inputs are finite; a program needn't handle non-finite values.
Results may differ from a plain program's by a relative error of at most 0.0003.
Values sent between devices are 32-bit elements.
A program may use at most 64 MiB of HBM per device.

v0:
```python
import jax
import jax.numpy as jnp
from jax import lax
from jax.sharding import PartitionSpec as P

LAYERS = 3


def count_bits(values, count):
    places = jnp.arange(count.bit_length() - 1, dtype=jnp.int32)
    return jnp.sum(values[..., None] >> places & 1, axis=-1)


def rotation_table(count, angle):
    rank = jnp.arange(count, dtype=jnp.int32)
    apart = count_bits(rank[:, None] ^ rank[None, :], count)
    bits = count.bit_length() - 1
    size = jnp.cos(angle) ** (bits - apart).astype(jnp.float32) * jnp.sin(angle) ** apart.astype(
        jnp.float32
    )
    real_sign = jnp.where(apart % 4 == 0, 1.0, jnp.where(apart % 4 == 2, -1.0, 0.0)).astype(
        jnp.float32
    )
    imag_sign = jnp.where(apart % 4 == 1, -1.0, jnp.where(apart % 4 == 3, 1.0, 0.0)).astype(
        jnp.float32
    )
    return (size * real_sign, size * imag_sign)


def mix_dim(values, dim, angle):
    real_part, imag_part = rotation_table(values.shape[dim], angle)

    def times(table):
        moved = jnp.tensordot(values, table, axes=([dim], [0]), precision=lax.Precision.HIGHEST)
        return jnp.moveaxis(moved, -1, dim)

    by_real = times(real_part)
    by_imag = times(imag_part)
    return jnp.stack([by_real[0] - by_imag[1], by_real[1] + by_imag[0]])


def phase_step(values, levels, angle):
    turn = angle * levels
    return jnp.stack(
        [
            values[0] * jnp.cos(turn) + values[1] * jnp.sin(turn),
            values[1] * jnp.cos(turn) - values[0] * jnp.sin(turn),
        ]
    )


def shards(wave_parts, level_table, diagonal_angles, turn_angles):
    values = wave_parts
    for layer in range(LAYERS):
        values = phase_step(values, level_table, diagonal_angles[layer])
        values = mix_dim(values, 3, turn_angles[layer, 0])
        values = mix_dim(values, 2, turn_angles[layer, 1])
        moved = lax.all_to_all(values, "qa", split_axis=2, concat_axis=1, tiled=True)
        moved = mix_dim(moved, 1, turn_angles[layer, 2])
        values = lax.all_to_all(moved, "qa", split_axis=1, concat_axis=2, tiled=True)
        moved = lax.all_to_all(values, "qb", split_axis=3, concat_axis=1, tiled=True)
        spread = moved.reshape(2, lax.axis_size("qb"), -1, moved.shape[2], moved.shape[3])
        moved = mix_dim(spread, 1, turn_angles[layer, 3]).reshape(moved.shape)
        values = lax.all_to_all(moved, "qb", split_axis=1, concat_axis=3, tiled=True)
    return values


def solution(mesh):
    placed = (
        P("trial", ("qa", "qb"), None, None),
        P(("trial", "qa", "qb"), None, None),
        P("trial", None),
        P("trial", None),
    )
    return jax.shard_map(
        shards,
        mesh=mesh,
        in_specs=placed,
        out_specs=P("trial", ("qa", "qb"), None, None),
        check_vma=False,
    )
```

profile of v0, /device:TPU:0, one launch (start us, length us, event | category | flops | bytes accessed | tf_op | source)
XLA Modules:
  0.0 201.9 jit_solution(17352092322198535005)
XLA Ops:
  0.0 1.8 fusion.327
  3.3 0.6 copy-done.1
  3.9 2.0 %fusion.19 = (f32[1,4,128,128]{3,2,1,0:T(8,128)S(1)}, f32[1,4,128,128]{3,2,1,0:T(8,128)S(1)}) fusion(f32[2,4,128,128]{3,2,1,0:T(8,128)} %param.4, f32[4,128,128]{2,1,0:T(8,128)} %param.5, f32[128]{0:T(128)S(1)} %get-tuple-element.54), kind=kLoop, calls=%fused_computation.79 | loop fusion | flops 458752 | bytes 1311232 | tf_op jit(solution)/shard_map/stack | solution.py:44
  6.0 0.8 fusion.17
  6.8 0.8 fusion.16
  9.1 1.1 convolution_bitcast_fusion.17
  10.2 1.1 convolution_bitcast_fusion.16
  11.4 1.0 copy.169
  12.4 5.2 %all-to-all-start = ((f32[2,4,128,128]{3,1,0,2:T(4,128)}), f32[2,4,128,128]{3,1,0,2:T(4,128)S(1)}, u32[]{:S(2)}, u32[]{:S(2)}) async-start(f32[2,4,128,128]{3,1,0,2:T(4,128)} %copy.169), calls=%async_computation | async-start | bytes 1048576 | tf_op jit(solution)/shard_map/all_to_all | solution.py:58
  19.0 6.6 %all-to-all-done = f32[2,4,128,128]{3,1,0,2:T(4,128)S(1)} async-done(((f32[2,4,128,128]{3,1,0,2:T(4,128)}), f32[2,4,128,128]{3,1,0,2:T(4,128)S(1)}, u32[]{:S(2)}, u32[]{:S(2)}) %all-to-all-start) | async-done | bytes 524320 | tf_op jit(solution)/shard_map/all_to_all | solution.py:58
  25.7 0.3 copy.171
  26.0 0.6 convolution_bitcast_fusion.15
  26.7 0.6 convolution_bitcast_fusion.14
  27.5 0.2 copy.174
  27.6 10.2 %all_to_all.201 = f32[2,16,32,128]{3,2,0,1:T(8,128)S(1)} all-to-all(f32[2,16,32,128]{3,2,0,1:T(8,128)S(1)} %copy.174), channel_id=1, replica_groups=mesh['trial'=2,'qa'=4,'qb'=4] {'qa'}, dimensions={1} | all-to-all | bytes 1048576 | tf_op jit(solution)/shard_map/all_to_all | solution.py:60
  37.9 1.0 copy.177
  38.9 4.9 %all-to-all-start.2 = ((f32[2,4,128,128]{2,1,0,3:T(4,128)}), f32[2,4,128,128]{2,1,0,3:T(4,128)S(1)}, u32[]{:S(2)}, u32[]{:S(2)}) async-start(f32[2,4,128,128]{2,1,0,3:T(4,128)} %copy.177), calls=%async_computation.2 | async-start | bytes 1048576 | tf_op jit(solution)/shard_map/all_to_all | solution.py:61
  45.1 10.7 %all-to-all-done.2 = f32[2,4,128,128]{2,1,0,3:T(4,128)S(1)} async-done(((f32[2,4,128,128]{2,1,0,3:T(4,128)}), f32[2,4,128,128]{2,1,0,3:T(4,128)S(1)}, u32[]{:S(2)}, u32[]{:S(2)}) %all-to-all-start.2) | async-done | bytes 524320 | tf_op jit(solution)/shard_map/all_to_all | solution.py:61
  55.7 1.3 convolution_bitcast_fusion.13
  57.1 1.3 convolution_bitcast_fusion.12
  58.7 0.8 copy.184
  59.5 3.7 %all-to-all-start.3 = ((f32[2,16,128,32]{2,3,0,1:T(8,128)}), f32[2,16,128,32]{2,3,0,1:T(8,128)S(1)}, u32[]{:S(2)}, u32[]{:S(2)}) async-start(f32[2,16,128,32]{2,3,0,1:T(8,128)} %copy.184), calls=%async_computation.3 | async-start | bytes 1048576 | tf_op jit(solution)/shard_map/all_to_all | solution.py:64
  66.2 8.8 %all-to-all-done.3 = f32[2,16,128,32]{2,3,0,1:T(8,128)S(1)} async-done(((f32[2,16,128,32]{2,3,0,1:T(8,128)}), f32[2,16,128,32]{2,3,0,1:T(8,128)S(1)}, u32[]{:S(2)}, u32[]{:S(2)}) %all-to-all-start.3) | async-done | bytes 524320 | tf_op jit(solution)/shard_map/all_to_all | solution.py:64
  75.4 0.8 copy-done
  76.2 1.0 add_bitcast_fusion.1
  77.2 0.8 fusion.15
  78.0 0.8 fusion.14
  78.8 1.1 convolution_bitcast_fusion.11
  79.9 1.1 convolution_bitcast_fusion.10
  81.1 1.0 copy.194
  82.1 3.5 %all-to-all-start.4 = ((f32[2,4,128,128]{3,1,0,2:T(4,128)}), f32[2,4,128,128]{3,1,0,2:T(4,128)S(1)}, u32[]{:S(2)}, u32[]{:S(2)}) async-start(f32[2,4,128,128]{3,1,0,2:T(4,128)} %copy.194), calls=%async_computation.4 | async-start | bytes 1048576 | tf_op jit(solution)/shard_map/all_to_all | solution.py:58
  86.9 5.3 %all-to-all-done.4 = f32[2,4,128,128]{3,1,0,2:T(4,128)S(1)} async-done(((f32[2,4,128,128]{3,1,0,2:T(4,128)}), f32[2,4,128,128]{3,1,0,2:T(4,128)S(1)}, u32[]{:S(2)}, u32[]{:S(2)}) %all-to-all-start.4) | async-done | bytes 524320 | tf_op jit(solution)/shard_map/all_to_all | solution.py:58
  92.3 0.3 copy.196
  92.6 0.6 convolution_bitcast_fusion.9
  93.3 0.6 convolution_bitcast_fusion.8
  94.0 0.2 copy.199
  94.2 9.7 %all_to_all.202 = f32[2,16,32,128]{3,2,0,1:T(8,128)S(1)} all-to-all(f32[2,16,32,128]{3,2,0,1:T(8,128)S(1)} %copy.199), channel_id=1, replica_groups=mesh['trial'=2,'qa'=4,'qb'=4] {'qa'}, dimensions={1} | all-to-all | bytes 1048576 | tf_op jit(solution)/shard_map/all_to_all | solution.py:60
  103.9 1.0 copy.202
  104.9 3.5 %all-to-all-start.6 = ((f32[2,4,128,128]{2,1,0,3:T(4,128)}), f32[2,4,128,128]{2,1,0,3:T(4,128)S(1)}, u32[]{:S(2)}, u32[]{:S(2)}) async-start(f32[2,4,128,128]{2,1,0,3:T(4,128)} %copy.202), calls=%async_computation.6 | async-start | bytes 1048576 | tf_op jit(solution)/shard_map/all_to_all | solution.py:61
  109.8 8.9 %all-to-all-done.6 = f32[2,4,128,128]{2,1,0,3:T(4,128)S(1)} async-done(((f32[2,4,128,128]{2,1,0,3:T(4,128)}), f32[2,4,128,128]{2,1,0,3:T(4,128)S(1)}, u32[]{:S(2)}, u32[]{:S(2)}) %all-to-all-start.6) | async-done | bytes 524320 | tf_op jit(solution)/shard_map/all_to_all | solution.py:61
  118.6 1.3 convolution_bitcast_fusion.7
  120.0 1.3 convolution_bitcast_fusion.6
  121.6 0.8 copy.209
  122.4 3.7 %all-to-all-start.7 = ((f32[2,16,128,32]{2,3,0,1:T(8,128)}), f32[2,16,128,32]{2,3,0,1:T(8,128)S(1)}, u32[]{:S(2)}, u32[]{:S(2)}) async-start(f32[2,16,128,32]{2,3,0,1:T(8,128)} %copy.209), calls=%async_computation.7 | async-start | bytes 1048576 | tf_op jit(solution)/shard_map/all_to_all | solution.py:64
  128.8 7.3 %all-to-all-done.7 = f32[2,16,128,32]{2,3,0,1:T(8,128)S(1)} async-done(((f32[2,16,128,32]{2,3,0,1:T(8,128)}), f32[2,16,128,32]{2,3,0,1:T(8,128)S(1)}, u32[]{:S(2)}, u32[]{:S(2)}) %all-to-all-start.7) | async-done | bytes 524320 | tf_op jit(solution)/shard_map/all_to_all | solution.py:64
  136.6 1.0 add_bitcast_fusion
  137.6 0.8 fusion.13
  138.4 0.8 fusion.12
  139.2 1.1 convolution_bitcast_fusion.5
  140.4 1.1 convolution_bitcast_fusion.4
  141.6 1.0 copy.219
  142.6 3.5 %all-to-all-start.8 = ((f32[2,4,128,128]{3,1,0,2:T(4,128)}), f32[2,4,128,128]{3,1,0,2:T(4,128)S(1)}, u32[]{:S(2)}, u32[]{:S(2)}) async-start(f32[2,4,128,128]{3,1,0,2:T(4,128)} %copy.219), calls=%async_computation.8 | async-start | bytes 1048576 | tf_op jit(solution)/shard_map/all_to_all | solution.py:58
  147.6 6.0 %all-to-all-done.8 = f32[2,4,128,128]{3,1,0,2:T(4,128)S(1)} async-done(((f32[2,4,128,128]{3,1,0,2:T(4,128)}), f32[2,4,128,128]{3,1,0,2:T(4,128)S(1)}, u32[]{:S(2)}, u32[]{:S(2)}) %all-to-all-start.8) | async-done | bytes 524320 | tf_op jit(solution)/shard_map/all_to_all | solution.py:58
  153.7 0.3 copy.221
  154.0 0.6 convolution_bitcast_fusion.3
  154.7 0.6 convolution_bitcast_fusion.2
  155.6 9.7 %all_to_all.203 = f32[2,16,32,128]{3,2,0,1:T(8,128)S(1)} all-to-all(f32[2,16,32,128]{3,2,0,1:T(8,128)S(1)} %copy.224), channel_id=1, replica_groups=mesh['trial'=2,'qa'=4,'qb'=4] {'qa'}, dimensions={1} | all-to-all | bytes 1048576 | tf_op jit(solution)/shard_map/all_to_all | solution.py:60
  165.4 1.0 copy.227
  166.4 3.5 %all-to-all-start.10 = ((f32[2,4,128,128]{2,1,0,3:T(4,128)}), f32[2,4,128,128]{2,1,0,3:T(4,128)S(1)}, u32[]{:S(2)}, u32[]{:S(2)}) async-start(f32[2,4,128,128]{2,1,0,3:T(4,128)} %copy.227), calls=%async_computation.10 | async-start | bytes 1048576 | tf_op jit(solution)/shard_map/all_to_all | solution.py:61
  171.2 11.3 %all-to-all-done.10 = f32[2,4,128,128]{2,1,0,3:T(4,128)S(1)} async-done(((f32[2,4,128,128]{2,1,0,3:T(4,128)}), f32[2,4,128,128]{2,1,0,3:T(4,128)S(1)}, u32[]{:S(2)}, u32[]{:S(2)}) %all-to-all-start.10) | async-done | bytes 524320 | tf_op jit(solution)/shard_map/all_to_all | solution.py:61
  182.5 1.3 convolution_bitcast_fusion.1
  183.8 1.3 convolution_bitcast_fusion
  185.4 15.4 %all_to_all.204 = f32[2,16,128,32]{2,3,0,1:T(8,128)S(1)} all-to-all(f32[2,16,128,32]{2,3,0,1:T(8,128)S(1)} %copy.234), channel_id=1, replica_groups=mesh['trial'=2,'qa'=4,'qb'=4] {'qb'}, dimensions={1} | all-to-all | bytes 1048576 | tf_op jit(solution)/shard_map/all_to_all | solution.py:64
  200.9 1.0 copy.237
  (59 shorter events, 2.9 us)
Async XLA Ops:
  3.2 0.7 copy-start.1
  12.4 13.2 %all-to-all-start = ((f32[2,4,128,128]{3,1,0,2:T(4,128)}), f32[2,4,128,128]{3,1,0,2:T(4,128)S(1)}, u32[]{:S(2)}, u32[]{:S(2)}) async-start(f32[2,4,128,128]{3,1,0,2:T(4,128)} %copy.169), calls=%async_computation | async-start | bytes 1048576 | tf_op jit(solution)/shard_map/all_to_all | solution.py:58
  38.9 16.9 %all-to-all-start.2 = ((f32[2,4,128,128]{2,1,0,3:T(4,128)}), f32[2,4,128,128]{2,1,0,3:T(4,128)S(1)}, u32[]{:S(2)}, u32[]{:S(2)}) async-start(f32[2,4,128,128]{2,1,0,3:T(4,128)} %copy.177), calls=%async_computation.2 | async-start | bytes 1048576 | tf_op jit(solution)/shard_map/all_to_all | solution.py:61
  59.5 15.4 %all-to-all-start.3 = ((f32[2,16,128,32]{2,3,0,1:T(8,128)}), f32[2,16,128,32]{2,3,0,1:T(8,128)S(1)}, u32[]{:S(2)}, u32[]{:S(2)}) async-start(f32[2,16,128,32]{2,3,0,1:T(8,128)} %copy.184), calls=%async_computation.3 | async-start | bytes 1048576 | tf_op jit(solution)/shard_map/all_to_all | solution.py:64
  75.2 1.0 copy-start
  82.1 10.0 %all-to-all-start.4 = ((f32[2,4,128,128]{3,1,0,2:T(4,128)}), f32[2,4,128,128]{3,1,0,2:T(4,128)S(1)}, u32[]{:S(2)}, u32[]{:S(2)}) async-start(f32[2,4,128,128]{3,1,0,2:T(4,128)} %copy.194), calls=%async_computation.4 | async-start | bytes 1048576 | tf_op jit(solution)/shard_map/all_to_all | solution.py:58
  104.9 13.7 %all-to-all-start.6 = ((f32[2,4,128,128]{2,1,0,3:T(4,128)}), f32[2,4,128,128]{2,1,0,3:T(4,128)S(1)}, u32[]{:S(2)}, u32[]{:S(2)}) async-start(f32[2,4,128,128]{2,1,0,3:T(4,128)} %copy.202), calls=%async_computation.6 | async-start | bytes 1048576 | tf_op jit(solution)/shard_map/all_to_all | solution.py:61
  122.4 13.7 %all-to-all-start.7 = ((f32[2,16,128,32]{2,3,0,1:T(8,128)}), f32[2,16,128,32]{2,3,0,1:T(8,128)S(1)}, u32[]{:S(2)}, u32[]{:S(2)}) async-start(f32[2,16,128,32]{2,3,0,1:T(8,128)} %copy.209), calls=%async_computation.7 | async-start | bytes 1048576 | tf_op jit(solution)/shard_map/all_to_all | solution.py:64
  142.6 11.0 %all-to-all-start.8 = ((f32[2,4,128,128]{3,1,0,2:T(4,128)}), f32[2,4,128,128]{3,1,0,2:T(4,128)S(1)}, u32[]{:S(2)}, u32[]{:S(2)}) async-start(f32[2,4,128,128]{3,1,0,2:T(4,128)} %copy.219), calls=%async_computation.8 | async-start | bytes 1048576 | tf_op jit(solution)/shard_map/all_to_all | solution.py:58
  166.4 16.1 %all-to-all-start.10 = ((f32[2,4,128,128]{2,1,0,3:T(4,128)}), f32[2,4,128,128]{2,1,0,3:T(4,128)S(1)}, u32[]{:S(2)}, u32[]{:S(2)}) async-start(f32[2,4,128,128]{2,1,0,3:T(4,128)} %copy.227), calls=%async_computation.10 | async-start | bytes 1048576 | tf_op jit(solution)/shard_map/all_to_all | solution.py:61
where the time goes:
time: 203 us; the launch traced here: 202 us
  waiting for transfers between devices  64.8 us (32%)
  blocking collectives  44.9 us (22%)
  starting transfers between devices  31.3 us (15%)
  matrix products  23.1 us (11%)
  between operations  17.5 us (9%)
  local copies, waits for them, and re-layouts  14.8 us (7%)
  other arithmetic  5.5 us (3%)
    all_to_all x3, waiting for transfers between devices, shards(): lax.all_to_all(values, 'qb', split_axis=3, concat_axis=1, tiled=True)  30.8 us
    all_to_all x3, blocking collectives, shards(): lax.all_to_all(moved, 'qa', split_axis=1, concat_axis=2, tiled=True)  29.5 us
    dot_general x24, matrix products, times(): jnp.tensordot(values, table, axes=([dim], [0]), precision=lax.Precision.H...  23.1 us
    all_to_all x3, waiting for transfers between devices, shards(): lax.all_to_all(values, 'qa', split_axis=2, concat_axis=1, tiled=True)  17.9 us
    all_to_all x2, waiting for transfers between devices, shards(): lax.all_to_all(moved, 'qb', split_axis=1, concat_axis=3, tiled=True)  16.1 us
    all_to_all x1, blocking collectives, shards(): lax.all_to_all(moved, 'qb', split_axis=1, concat_axis=3, tiled=True)  15.4 us
    all_to_all x3, starting transfers between devices, shards(): lax.all_to_all(values, 'qa', split_axis=2, concat_axis=1, tiled=True)  12.2 us
    all_to_all x3, starting transfers between devices, shards(): lax.all_to_all(values, 'qb', split_axis=3, concat_axis=1, tiled=True)  11.8 us
  transfers between devices with their start and end apart: 8, of which 8 were waited for; matrix products, arithmetic and copies ran while one was open for 0% of the time, Pallas kernels for 0%

commit v1 on v0

--- a/solution.py
+++ b/solution.py
@@ -1,6 +1,10 @@
+import functools
+
 import jax
 import jax.numpy as jnp
 from jax import lax
+from jax.experimental import pallas as pl
+from jax.experimental.pallas import tpu as pltpu
 from jax.sharding import PartitionSpec as P
 
 LAYERS = 3
@@ -47,6 +51,304 @@
             values[1] * jnp.cos(turn) - values[0] * jnp.sin(turn),
         ]
     )
+
+
+def cos_sin(turn):
+    half = 0.5 * turn
+    y = half * half
+    sine = -1 / 39916800
+    for term in (1 / 362880, -1 / 5040, 1 / 120, -1 / 6, 1.0):
+        sine = sine * y + term
+    sine = sine * half
+    cosine = 1 / 479001600
+    for term in (-1 / 3628800, 1 / 40320, -1 / 720, 1 / 24, -0.5, 1.0):
+        cosine = cosine * y + term
+    return 1.0 - 2.0 * sine * sine, 2.0 * sine * cosine
+
+
+def split(x):
+    high = x.astype(jnp.bfloat16)
+    return high, (x - high.astype(jnp.float32)).astype(jnp.bfloat16)
+
+
+def times(a, b):
+    dot = functools.partial(jnp.dot, preferred_element_type=jnp.float32)
+    return dot(a[0], b[0]) + (dot(a[0], b[1]) + dot(a[1], b[0]))
+
+
+def moved_bits(fields, order):
+    def places(names):
+        at, low = {}, 0
+        for name in reversed(names):
+            at[name] = low
+            low += fields[name][0]
+        return at
+
+    into, out = places(order[0]), places(order[1])
+    return [
+        (out[name] + i, into[name] + i, group)
+        for name, (bits, group) in fields.items()
+        for i in range(bits)
+    ]
+
+
+def turn_table(size, bits, angles, out_axis):
+    out = lax.broadcasted_iota(jnp.int32, (size, size), out_axis)
+    into = lax.broadcasted_iota(jnp.int32, (size, size), 1 - out_axis)
+    table = None
+    for out_at, in_at, group in bits:
+        o = (out >> out_at) & 1
+        i = (into >> in_at) & 1
+        if group is None:
+            factor = jnp.where(o == i, 1.0, 0.0)
+        else:
+            c, s = angles[group]
+            factor = jnp.where(o == i, c, jnp.where(o > i, -s, s))
+        table = factor if table is None else table * factor
+    return table
+
+
+def mix_list(xs, groups, angles):
+    xs = list(xs)
+    step = len(xs)
+    for group in groups:
+        c, s = angles[group]
+        step //= 2
+        for j in range(len(xs)):
+            if not j & step:
+                u, v = xs[j], xs[j + step]
+                xs[j], xs[j + step] = c * u + s * v, c * v - s * u
+    return xs
+
+
+def log2(count):
+    return count.bit_length() - 1
+
+
+def kernel(na, nb, wave, level, diag, turns, out, x1, s1, r1, x2, s2, r2, x3, s3, r3,
+           tb, tp, tc, cs, send_sem, recv_sem, own_sem):
+    n = na * nb
+    blocks, rows, lanes = wave.shape[1:]
+    high = n // blocks
+    rest = rows // high
+    low = rest // n
+    f32 = jnp.float32
+    a = lax.axis_index("qa")
+    b = lax.axis_index("qb")
+    me = a * nb + b
+
+    def where_is(k):
+        peer = lax.rem(me + k, n)
+        return peer, {"qa": lax.div(peer, nb), "qb": lax.rem(peer, nb)}
+
+    barrier = pltpu.get_barrier_semaphore()
+
+    def greet(k, carry):
+        pl.semaphore_signal(barrier, inc=1, device_id=where_is(k)[1], device_id_type=pl.DeviceIdType.MESH)
+        return carry
+
+    lax.fori_loop(1, n, greet, 0)
+
+    def remote(src, dst, which, k):
+        peer, to = where_is(k)
+        return pltpu.make_async_remote_copy(
+            src_ref=src(peer), dst_ref=dst(me), send_sem=send_sem.at[which, k],
+            recv_sem=recv_sem.at[which, k], device_id=to, device_id_type=pl.DeviceIdType.MESH)
+
+    def send(src, dst, which):
+        def one(k, carry):
+            remote(src, dst, which, k).start()
+            return carry
+
+        lax.fori_loop(1, n, one, 0)
+        pltpu.make_async_copy(src(me), dst(me), own_sem.at[which]).start()
+
+    def arrive(src, dst, which):
+        def one(k, carry):
+            remote(src, dst, which, k).wait_recv()
+            return carry
+
+        lax.fori_loop(1, n, one, 0)
+        pltpu.make_async_copy(src(me), dst(me), own_sem.at[which]).wait()
+
+    def sent(src, dst, which):
+        def one(k, carry):
+            remote(src, dst, which, k).wait_send()
+            return carry
+
+        lax.fori_loop(1, n, one, 0)
+
+    plans = []
+    for p in range(2):
+        plans.append((lambda i, p=p: s1.at[p, i], lambda i, p=p: r1.at[p, i], p))
+    for p in range(2):
+        plans.append((lambda i, p=p: s2.at[p, :, i], lambda i, p=p: r2.at[p, i], 2 + p))
+    for p in range(2):
+        plans.append((lambda i, p=p: s3.at[p, i], lambda i, p=p: r3.at[p, i], 4 + p))
+    per = n // blocks
+    table_b = (lambda i: level.at[i // per, pl.ds(pl.multiple_of((i % per) * rest, 8), rest)], lambda i: tb.at[i], 6)
+    table_c = (lambda i: tp.at[:, i], lambda i: tc.at[i], 7)
+
+    angles = []
+    for layer in range(LAYERS):
+        angles.append([cos_sin(jnp.full((1, lanes), turns[layer, g], f32)) for g in range(4)])
+    lane_bits = [(i, i, 0) for i in range(log2(lanes))]
+
+    row_at = lax.broadcasted_iota(jnp.int32, (rows, lanes), 0)
+    lane_at = lax.broadcasted_iota(jnp.int32, (rows, lanes), 1)
+    ones = jnp.zeros((rows, lanes), jnp.int32)
+    for i in range(log2(rows)):
+        ones = ones + ((row_at >> i) & 1)
+    for i in range(log2(lanes)):
+        ones = ones + ((lane_at >> i) & 1)
+    for i in range(log2(n)):
+        ones = ones + lax.rem(lax.div(me, 1 << i), 2)
+
+    def power(block):
+        q = (ones + block.bit_count()) & 3
+        real = jnp.where(q == 0, 1.0, jnp.where(q == 2, -1.0, 0.0))
+        imag = jnp.where(q == 1, -1.0, jnp.where(q == 3, 1.0, 0.0))
+        return real, imag
+
+    for g in range(blocks):
+        c, s = cos_sin(diag[0:1, :] * level[g])
+        re, im = wave[0, g], wave[1, g]
+        re, im = re * c + im * s, im * c - re * s
+        fr, fi = power(g)
+        x1[0, g] = re * fr - im * fi
+        x1[1, g] = im * fr + re * fi
+
+    pl.semaphore_wait(barrier, n - 1)
+    send(*table_b)
+
+    def segment(layer, bits, take, put, plan):
+        turn = angles[layer]
+        right = split(turn_table(lanes, lane_bits, turn, 1))
+        left = split(turn_table(rows, bits, turn, 0))
+        for p in range(2):
+            xs = [times(left, split(times(split(take(p, g)), right))) for g in range(blocks)]
+            for g, x in enumerate(mix_list(xs, [2] * log2(blocks), turn)):
+                put(p, g, x)
+            send(*plan[p])
+
+    def join(received, table, layer, groups, take, put, plan, count):
+        def phase(j, carry):
+            c, s = cos_sin(diag[layer + 1 : layer + 2, :] * take(table, j))
+            cs[0, j] = c
+            cs[1, j] = s
+            return carry
+
+        lax.fori_loop(0, count, phase, 0)
+        arrive(*plan[0])
+        arrive(*plan[1])
+
+        def step(j, carry):
+            re = mix_list(take(received.at[0], j), groups, angles[layer])
+            im = mix_list(take(received.at[1], j), groups, angles[layer])
+            for i in range(n):
+                c, s = cs[0, j, i], cs[1, j, i]
+                put(0, i, j, re[i] * c + im[i] * s)
+                put(1, i, j, im[i] * c - re[i] * s)
+            return carry
+
+        lax.fori_loop(0, count, step, 0)
+
+    def put1(p, g, x):
+        s1[p, g * per : (g + 1) * per] = x.reshape(per, rest, lanes)
+
+    segment(0, [(i, i, 1) for i in range(log2(rows))], lambda p, g: x1[p, g], put1, plans[0:2])
+
+    arrive(*table_b)
+    fields_b = dict(b=(log2(nb), 3), mid=(log2(n), 1), low=(log2(low), 1))
+    orders_b = (("b", "mid", "low"), ("mid", "b", "low"))
+    bits_b = moved_bits(fields_b, orders_b)
+    place = turn_table(rows, [(o, i, None) for o, i, _ in bits_b], None, 0).astype(jnp.bfloat16)
+    for g in range(na):
+        x = tb[g * nb : (g + 1) * nb].reshape(rows, lanes)
+        first = x.astype(jnp.bfloat16)
+        x = x - first.astype(f32)
+        second = x.astype(jnp.bfloat16)
+        third = (x - second.astype(f32)).astype(jnp.bfloat16)
+        first, second, third = [jnp.dot(place, y, preferred_element_type=f32) for y in (first, second, third)]
+        tp[g] = ((first + second) + third).reshape(n, nb * low, lanes)
+    send(*table_c)
+
+    def take_b(ref, j):
+        return ref[:, pl.ds(pl.multiple_of(j * 8, 8), 8), :]
+
+    def put_b(p, i, j, x):
+        x2[p, i, pl.ds(pl.multiple_of(j * 8, 8), 8), :] = x
+
+    join(r1, tb, 0, [2] * log2(na) + [3] * log2(nb), take_b, put_b, plans[0:2], rest // 8)
+
+    def put2(p, g, x):
+        s2[p, g] = x.reshape(n, nb * low, lanes)
+
+    segment(1, bits_b, lambda p, g: x2[p, g * nb : (g + 1) * nb].reshape(rows, lanes), put2, plans[2:4])
+
+    arrive(*table_c)
+
+    def put_c(p, i, j, x):
+        x3[p, i, j] = x
+
+    join(r2, tc, 1, [2] * log2(blocks) + [1] * log2(high), lambda ref, j: ref[:, j], put_c, plans[2:4], na)
+
+    fields_c = dict(block=(log2(blocks), 2), high=(log2(high), 1), b=(log2(nb), 3), low=(log2(low), 1))
+    bits_c = moved_bits(fields_c, (("block", "high", "b", "low"), ("b", "block", "high", "low")))
+
+    def put3(p, g, x):
+        s3[p, g * nb : (g + 1) * nb] = x.reshape(nb, blocks, high * low, lanes)
+
+    segment(2, bits_c, lambda p, g: x3[p, :, g].reshape(rows, lanes), put3, plans[4:6])
+
+    fields_a = dict(mid=(log2(n), 1), high=(log2(high), None), low=(log2(low), None))
+    bits_a = moved_bits(fields_a, (("mid", "high", "low"), ("high", "mid", "low")))
+    last = split(turn_table(rows, bits_a, angles[2], 0))
+    arrive(*plans[4])
+    arrive(*plans[5])
+    for g in range(blocks):
+        re, im = [times(last, split(r3[p, :, g].reshape(rows, lanes))) for p in range(2)]
+        fr, fi = power(g)
+        out[0, g] = re * fr + im * fi
+        out[1, g] = im * fr - re * fi
+    for plan in plans + [table_b, table_c]:
+        sent(*plan)
+
+
+def fits(na, nb, blocks, rows):
+    n = na * nb
+    if blocks != na or n % blocks or rows * blocks % (n * n):
+        return False
+    high = n // blocks
+    low = rows // high // n
+    return nb * low == 8 and high * low == 8
+
+
+def fused(wave_parts, level_table, diagonal_angles, turn_angles, na, nb):
+    n = na * nb
+    _, blocks, rows, lanes = wave_parts.shape
+    rest = rows * blocks // n
+    f32 = jnp.float32
+    V = pltpu.VMEM
+    flat = V((2, n, rest, lanes), f32)
+    tiles = V((2, n, na, 8, lanes), f32)
+    vmem = pl.BlockSpec(memory_space=pltpu.VMEM)
+    return pl.pallas_call(
+        functools.partial(kernel, na, nb),
+        out_shape=jax.ShapeDtypeStruct(wave_parts.shape, f32),
+        in_specs=[vmem, vmem, vmem, pl.BlockSpec(memory_space=pltpu.SMEM)],
+        out_specs=vmem,
+        scratch_shapes=[
+            V(wave_parts.shape, f32), flat, flat,
+            flat, V((2, na, n, 8, lanes), f32), tiles,
+            tiles, V((2, n, blocks, 8, lanes), f32), V((2, n, blocks, 8, lanes), f32),
+            V((n, rest, lanes), f32), V((na, n, 8, lanes), f32), V((n, na, 8, lanes), f32),
+            V((2, na, n, 8, lanes), f32),
+            pltpu.SemaphoreType.DMA((8, n)), pltpu.SemaphoreType.DMA((8, n)), pltpu.SemaphoreType.DMA((8,)),
+        ],
+        compiler_params=pltpu.CompilerParams(
+            collective_id=0, has_side_effects=True, vmem_limit_bytes=32 * 1024 * 1024),
+    )(wave_parts, level_table, diagonal_angles, turn_angles)
 
 
 def shards(wave_parts, level_table, diagonal_angles, turn_angles):
@@ -66,6 +368,14 @@
 
 
 def solution(mesh):
+    na, nb = mesh.shape["qa"], mesh.shape["qb"]
+
+    def each(wave_parts, level_table, diagonal_angles, turn_angles):
+        args = (wave_parts, level_table, diagonal_angles, turn_angles)
+        if fits(na, nb, wave_parts.shape[1], wave_parts.shape[2]):
+            return fused(*args, na, nb)
+        return shards(*args)
+
     placed = (
         P("trial", ("qa", "qb"), None, None),
         P(("trial", "qa", "qb"), None, None),
@@ -73,7 +383,7 @@
         P("trial", None),
     )
     return jax.shard_map(
-        shards,
+        each,
         mesh=mesh,
         in_specs=placed,
         out_specs=P("trial", ("qa", "qb"), None, None),

time: 203 us -> 66.1 us (0.33)
  waiting for transfers between devices: 64.8 us -> 0 us
  Pallas kernels: 0 us -> 61.7 us
  blocking collectives: 44.9 us -> 0 us
  starting transfers between devices: 31.3 us -> 0 us
  matrix products: 23.1 us -> 0 us
  between operations: 17.5 us -> 0.01 us
  local copies, waits for them, and re-layouts: 14.8 us -> 4.15 us
  other arithmetic: 5.5 us -> 0 us
    all_to_all x8 -> x0, waiting for transfers between devices: 64.8 us -> none  [the longest x3 30.8 us: shards(): lax.all_to_all(values, 'qb', split_axis=3, concat_axis=1, tiled=True)]
    pallas_call x0 -> x1, Pallas kernels: none -> 61.7 us  [fused(): pl.pallas_call(functools.partial(kernel, na, nb), out_shape=jax.ShapeDtyp...]
    all_to_all x4 -> x0, blocking collectives: 44.9 us -> none  [the longest x3 29.5 us: shards(): lax.all_to_all(moved, 'qa', split_axis=1, concat_axis=2, tiled=True)]
    all_to_all x8 -> x0, starting transfers between devices: 31.3 us -> none  [the longest x3 12.2 us: shards(): lax.all_to_all(values, 'qa', split_axis=2, concat_axis=1, tiled=True)]
    dot_general x24 -> x0, matrix products: 23.1 us -> none  [times(): jnp.tensordot(values, table, axes=([dim], [0]), precision=lax.Precision.H...]
    all_to_all x16 -> x0, local copies, waits for them, and re-layouts: 5.52 us -> none  [the longest x6 3.09 us: shards(): lax.all_to_all(moved, 'qa', split_axis=1, concat_axis=2, tiled=True)]
    another operation x9 -> x0, local copies, waits for them, and re-layouts: 5.21 us -> none  [mix_dim(): return jnp.stack([by_real[0] - by_imag[1], by_real[1] + by_imag[0]])]
    another operation x12 -> x0, other arithmetic: 4.41 us -> none  [the longest x3 4.08 us: phase_step(): jnp.stack([values[0] * jnp.cos(turn) + values[1] * jnp.sin(turn), values[...]
  transfers between devices with their start and end apart: 8 -> 0, of which waited for: 8 -> 0; matrix products, arithmetic and copies ran while one was open for 0% -> 0% of each run, Pallas kernels for 0% -> 0%
where the time goes in v1:
time: 66.1 us; the launch traced here: 65.8 us
  Pallas kernels  61.7 us (93%)
  local copies, waits for them, and re-layouts  4.15 us (6%)
    pallas_call x1, Pallas kernels, fused(): pl.pallas_call(functools.partial(kernel, na, nb), out_shape=jax.ShapeDtyp...  61.7 us
    unnamed x9, local copies, waits for them, and re-layouts  4.15 us

profile of v1, /device:TPU:0, one launch (start us, length us, event | category | flops | bytes accessed | tf_op | source)
XLA Modules:
  0.0 65.8 jit_solution(15490380894570090706)
XLA Ops:
  0.0 0.0 copy-start
  0.0 1.0 %copy-done = f32[2,4,128,128]{3,2,1,0:T(8,128)S(1)} copy-done((f32[2,4,128,128]{3,2,1,0:T(8,128)S(1)}, f32[2,4,128,128]{3,2,1,0:T(8,128)}, u32[]{:S(2)}) %copy-start) | copy-done | bytes 524312
  1.0 0.0 copy-start.1
  1.0 0.9 %copy-done.1 = f32[4,128,128]{2,1,0:T(8,128)S(1)} copy-done((f32[4,128,128]{2,1,0:T(8,128)S(1)}, f32[4,128,128]{2,1,0:T(8,128)}, u32[]{:S(2)}) %copy-start.1) | copy-done | bytes 262168
  2.0 0.0 copy-start.2
  2.0 0.7 %copy-done.2 = f32[3,128]{1,0:T(4,128)S(1)} copy-done((f32[3,128]{1,0:T(4,128)S(1)}, f32[3,128]{1,0:T(4,128)}, u32[]{:S(2)}) %copy-start.2) | copy-done | bytes 1560
  2.7 0.0 copy-start.3
  2.7 0.7 %copy-done.3 = f32[3,4]{1,0:T(4,128)S(1)} copy-done((f32[3,4]{1,0:T(4,128)S(1)}, f32[3,4]{1,0:T(4,128)}, u32[]{:S(2)}) %copy-start.3) | copy-done | bytes 72
  3.4 61.7 %shard_map.46 = f32[2,4,128,128]{3,2,1,0:T(8,128)S(1)} custom-call(f32[2,4,128,128]{3,2,1,0:T(8,128)S(1)} %copy-done, f32[4,128,128]{2,1,0:T(8,128)S(1)} %copy-done.1, f32[3,128]{1,0:T(4,128)S(1)} %copy-done.2, f32[3,4]{1,0:T(4,128)S(1)} %copy-done.3), custom_call_target="tpu_custom_call" | custom-call | tf_op jit(solution)/shard_map/pallas_call | solution.py:336
  65.0 0.8 %copy.6 = f32[2,4,128,128]{3,2,1,0:T(8,128)} copy(f32[2,4,128,128]{3,2,1,0:T(8,128)S(1)} %shard_map.46) | data formatting | bytes 1048576
Async XLA Ops:
  0.0 1.0 %copy-start = (f32[2,4,128,128]{3,2,1,0:T(8,128)S(1)}, f32[2,4,128,128]{3,2,1,0:T(8,128)}, u32[]{:S(2)}) copy-start(f32[2,4,128,128]{3,2,1,0:T(8,128)} %wave.1) | copy-start | bytes 1572868
  1.0 0.9 %copy-start.1 = (f32[4,128,128]{2,1,0:T(8,128)S(1)}, f32[4,128,128]{2,1,0:T(8,128)}, u32[]{:S(2)}) copy-start(f32[4,128,128]{2,1,0:T(8,128)} %level.1) | copy-start | bytes 786436
  2.0 0.7 %copy-start.2 = (f32[3,128]{1,0:T(4,128)S(1)}, f32[3,128]{1,0:T(4,128)}, u32[]{:S(2)}) copy-start(f32[3,128]{1,0:T(4,128)} %diag.1) | copy-start | bytes 4612
  2.7 0.7 %copy-start.3 = (f32[3,4]{1,0:T(4,128)S(1)}, f32[3,4]{1,0:T(4,128)}, u32[]{:S(2)}) copy-start(f32[3,4]{1,0:T(4,128)} %turns.1) | copy-start | bytes 148

commit v2 on v1

--- a/solution.py
+++ b/solution.py
@@ -137,17 +137,22 @@
     b = lax.axis_index("qb")
     me = a * nb + b
 
+    def flipped(x, mask):
+        for i in range(log2(n)):
+            if mask >> i & 1:
+                x = x + (1 << i) * (1 - 2 * lax.rem(lax.div(x, 1 << i), 2))
+        return x
+
     def where_is(k):
-        peer = lax.rem(me + k, n)
-        return peer, {"qa": lax.div(peer, nb), "qb": lax.rem(peer, nb)}
+        pa, pb = flipped(a, k // nb), flipped(b, k % nb)
+        return pa * nb + pb, {"qa": pa, "qb": pb}
+
+    masks = sorted(range(1, n), key=lambda k: (-(k % nb), -(k // nb)))
 
     barrier = pltpu.get_barrier_semaphore()
 
-    def greet(k, carry):
+    for k in masks:
         pl.semaphore_signal(barrier, inc=1, device_id=where_is(k)[1], device_id_type=pl.DeviceIdType.MESH)
-        return carry
-
-    lax.fori_loop(1, n, greet, 0)
 
     def remote(src, dst, which, k):
         peer, to = where_is(k)
@@ -156,27 +161,18 @@
             recv_sem=recv_sem.at[which, k], device_id=to, device_id_type=pl.DeviceIdType.MESH)
 
     def send(src, dst, which):
-        def one(k, carry):
+        for k in masks:
             remote(src, dst, which, k).start()
-            return carry
-
-        lax.fori_loop(1, n, one, 0)
         pltpu.make_async_copy(src(me), dst(me), own_sem.at[which]).start()
 
     def arrive(src, dst, which):
-        def one(k, carry):
+        for k in masks:
             remote(src, dst, which, k).wait_recv()
-            return carry
-
-        lax.fori_loop(1, n, one, 0)
         pltpu.make_async_copy(src(me), dst(me), own_sem.at[which]).wait()
 
     def sent(src, dst, which):
-        def one(k, carry):
+        for k in masks:
             remote(src, dst, which, k).wait_send()
-            return carry
-
-        lax.fori_loop(1, n, one, 0)
 
     plans = []
     for p in range(2):
@@ -210,6 +206,9 @@
         imag = jnp.where(q == 1, -1.0, jnp.where(q == 3, 1.0, 0.0))
         return real, imag
 
+    pl.semaphore_wait(barrier, n - 1)
+    send(*table_b)
+
     for g in range(blocks):
         c, s = cos_sin(diag[0:1, :] * level[g])
         re, im = wave[0, g], wave[1, g]
@@ -217,9 +216,6 @@
         fr, fi = power(g)
         x1[0, g] = re * fr - im * fi
         x1[1, g] = im * fr + re * fi
-
-    pl.semaphore_wait(barrier, n - 1)
-    send(*table_b)
 
     def segment(layer, bits, take, put, plan):
         turn = angles[layer]
@@ -240,6 +236,8 @@
 
         lax.fori_loop(0, count, phase, 0)
         arrive(*plan[0])
+        if layer == 0:
+            send(*table_c)
         arrive(*plan[1])
 
         def step(j, carry):
@@ -271,8 +269,6 @@
         third = (x - second.astype(f32)).astype(jnp.bfloat16)
         first, second, third = [jnp.dot(place, y, preferred_element_type=f32) for y in (first, second, third)]
         tp[g] = ((first + second) + third).reshape(n, nb * low, lanes)
-    send(*table_c)
-
     def take_b(ref, j):
         return ref[:, pl.ds(pl.multiple_of(j * 8, 8), 8), :]
 

time: 66.1 us -> 62.7 us (0.949)
  Pallas kernels: 61.7 us -> 58.3 us
    pallas_call x1, Pallas kernels: 61.7 us -> 58.3 us  [fused(): pl.pallas_call(functools.partial(kernel, na, nb), out_shape=jax.ShapeDtyp...]
where the time goes in v2:
time: 62.7 us; the launch traced here: 62.4 us
  Pallas kernels  58.3 us (93%)
  local copies, waits for them, and re-layouts  4.15 us (7%)
    pallas_call x1, Pallas kernels, fused(): pl.pallas_call(functools.partial(kernel, na, nb), out_shape=jax.ShapeDtyp...  58.3 us
    unnamed x9, local copies, waits for them, and re-layouts  4.15 us

profile of v2, /device:TPU:0, one launch (start us, length us, event | category | flops | bytes accessed | tf_op | source)
XLA Modules:
  0.0 62.4 jit_solution(5432048679351222492)
XLA Ops:
  0.0 0.0 copy-start
  0.0 1.0 %copy-done = f32[2,4,128,128]{3,2,1,0:T(8,128)S(1)} copy-done((f32[2,4,128,128]{3,2,1,0:T(8,128)S(1)}, f32[2,4,128,128]{3,2,1,0:T(8,128)}, u32[]{:S(2)}) %copy-start) | copy-done | bytes 524312
  1.0 0.0 copy-start.1
  1.0 0.9 %copy-done.1 = f32[4,128,128]{2,1,0:T(8,128)S(1)} copy-done((f32[4,128,128]{2,1,0:T(8,128)S(1)}, f32[4,128,128]{2,1,0:T(8,128)}, u32[]{:S(2)}) %copy-start.1) | copy-done | bytes 262168
  2.0 0.0 copy-start.2
  2.0 0.7 %copy-done.2 = f32[3,128]{1,0:T(4,128)S(1)} copy-done((f32[3,128]{1,0:T(4,128)S(1)}, f32[3,128]{1,0:T(4,128)}, u32[]{:S(2)}) %copy-start.2) | copy-done | bytes 1560
  2.7 0.0 copy-start.3
  2.7 0.7 %copy-done.3 = f32[3,4]{1,0:T(4,128)S(1)} copy-done((f32[3,4]{1,0:T(4,128)S(1)}, f32[3,4]{1,0:T(4,128)}, u32[]{:S(2)}) %copy-start.3) | copy-done | bytes 72
  3.4 58.3 %shard_map.46 = f32[2,4,128,128]{3,2,1,0:T(8,128)S(1)} custom-call(f32[2,4,128,128]{3,2,1,0:T(8,128)S(1)} %copy-done, f32[4,128,128]{2,1,0:T(8,128)S(1)} %copy-done.1, f32[3,128]{1,0:T(4,128)S(1)} %copy-done.2, f32[3,4]{1,0:T(4,128)S(1)} %copy-done.3), custom_call_target="tpu_custom_call" | custom-call | tf_op jit(solution)/shard_map/pallas_call | solution.py:332
  61.6 0.8 %copy.6 = f32[2,4,128,128]{3,2,1,0:T(8,128)} copy(f32[2,4,128,128]{3,2,1,0:T(8,128)S(1)} %shard_map.46) | data formatting | bytes 1048576
Async XLA Ops:
  0.0 1.0 %copy-start = (f32[2,4,128,128]{3,2,1,0:T(8,128)S(1)}, f32[2,4,128,128]{3,2,1,0:T(8,128)}, u32[]{:S(2)}) copy-start(f32[2,4,128,128]{3,2,1,0:T(8,128)} %wave.1) | copy-start | bytes 1572868
  1.0 0.9 %copy-start.1 = (f32[4,128,128]{2,1,0:T(8,128)S(1)}, f32[4,128,128]{2,1,0:T(8,128)}, u32[]{:S(2)}) copy-start(f32[4,128,128]{2,1,0:T(8,128)} %level.1) | copy-start | bytes 786436
  2.0 0.7 %copy-start.2 = (f32[3,128]{1,0:T(4,128)S(1)}, f32[3,128]{1,0:T(4,128)}, u32[]{:S(2)}) copy-start(f32[3,128]{1,0:T(4,128)} %diag.1) | copy-start | bytes 4612
  2.7 0.7 %copy-start.3 = (f32[3,4]{1,0:T(4,128)S(1)}, f32[3,4]{1,0:T(4,128)}, u32[]{:S(2)}) copy-start(f32[3,4]{1,0:T(4,128)} %turns.1) | copy-start | bytes 148
